TPU v7x, 128 devices: a whole 4x4x4 slice. The times are simulated.
128 devices in a mesh: lat: 32 (over z, x, core), lev: 4 (over y).
Axes of the slice: x: 4, y: 4, z: 4, core: 2. Of those that a mesh axis runs over, the one named last changes fastest.
Arguments:
- grid: bfloat16 [640, 128, 4, 1280], P('lat', 'lev'), may hold values from -6 to 6
- legendre: bfloat16 [640, 640, 640], P('lat'), may hold values from -0.25 to 0.25
- vertical: bfloat16 [128, 128], P('lev'), may hold values from -0.5 to 0.5
- damping: bfloat16 [128], P('lev'), may hold values from 1 to 16
- lon_counts: int32 [640], replicated, may hold values from 160 to 1280
- wave_slots: int32 [640], replicated, may hold values from 0 to 639, as said below
Outputs:
- filtered_grid: bfloat16 [640, 128, 4, 1280], P('lat', 'lev')
Inputs may be any that keep to these rules, and one draw needn't show every extreme that they name: wave_slots is a permutation; slot g * 5 + r holds a wavenumber from r * 128 to (r + 1) * 128 - 1.
All inputs are finite; a program needn't handle non-finite values.
Results may differ from a plain program's by a relative error of at most 0.0074.
Values may be sent and summed in bfloat16 or wider, within the bound.
A program may use at most 128 MiB of HBM per device.

v0:
```python
import math
import jax
import jax.numpy as jnp
from jax import lax
from jax.sharding import PartitionSpec as P


def sent_together(arrays, axis, dim, along):
    widths = [math.prod(a.shape[along:]) for a in arrays]
    both = jnp.concatenate(
        [a.reshape(*a.shape[:along], w) for a, w in zip(arrays, widths)], axis=along
    )
    result = lax.all_gather(both, axis, axis=dim, tiled=True)
    pieces = jnp.split(result, [sum(widths[:k]) for k in range(1, len(widths))], axis=along)
    return tuple(
        (b.reshape(*result.shape[:along], *a.shape[along:]) for a, b in zip(arrays, pieces))
    )


def in_blocks(array, dim, peers):
    before, after = (array.shape[:dim], array.shape[dim + 1 :])
    return jnp.moveaxis(array.reshape(*before, peers, -1, *after), dim, 0)


def in_order(pieces, dim):
    lengths = list(pieces.shape[1:])
    lengths[dim] *= pieces.shape[0]
    return jnp.moveaxis(pieces, 0, dim).reshape(lengths)


def joined_exchange(array, axis, axes, splits, concats):
    sizes = [lax.axis_size(a) for a in axes]
    pieces = in_blocks(array, splits[0], sizes[0])
    pieces = jnp.moveaxis(in_blocks(pieces, splits[1] + 1, sizes[1]), 0, 1)
    inside = pieces.shape[2:]
    pieces = pieces.reshape(-1, *inside)
    pieces = lax.all_to_all(pieces, axis, split_axis=0, concat_axis=0, tiled=True)
    pieces = in_order(pieces.reshape(*sizes, *inside), concats[0] + 1)
    return in_order(pieces, concats[1])


def forward_build(wavenumbers, longitudes):
    points = jnp.arange(longitudes, dtype=jnp.int32)
    phase = (wavenumbers[:, None] * points[None, :] % longitudes).astype(jnp.float32) * (
        2.0 * math.pi / longitudes
    )
    scale = 1.0 / math.sqrt(longitudes)
    return jnp.stack([jnp.cos(phase) * scale, -jnp.sin(phase) * scale], axis=1).astype(jnp.bfloat16)


def inverse_build(wavenumbers, longitudes):
    points = jnp.arange(longitudes, dtype=jnp.int32)
    phase = (wavenumbers[:, None] * points[None, :] % longitudes).astype(jnp.float32) * (
        2.0 * math.pi / longitudes
    )
    scale = 1.0 / math.sqrt(longitudes)
    weight = jnp.where(wavenumbers == 0, 1.0, 2.0).astype(jnp.float32)[:, None]
    return jnp.stack(
        [jnp.cos(phase) * scale * weight, -jnp.sin(phase) * scale * weight], axis=1
    ).astype(jnp.bfloat16)


def damping_factor(degrees, damping):
    degree_values = jnp.arange(degrees).astype(jnp.float32)
    ratio = degree_values * (degree_values + 1.0) / float(degrees * (degrees - 1))
    return 1.0 / (1.0 + damping.astype(jnp.float32)[None, :] * (ratio * ratio)[:, None])


def legendre_forward(table, fourier, wavenumbers):
    degrees = table.shape[1]
    spectral = jnp.einsum("sna,srac->snrc", table, fourier, preferred_element_type=jnp.float32)
    live = (jnp.arange(degrees, dtype=jnp.int32)[None, :] >= wavenumbers[:, None]).astype(
        jnp.float32
    )
    return (spectral * live[:, :, None, None]).astype(jnp.bfloat16)


def legendre_inverse(table, mixed):
    banded = jnp.einsum("sna,snrc->srac", table, mixed, preferred_element_type=jnp.float32)
    return banded.astype(jnp.bfloat16)


def per_device(grid, legendre, vertical, damping, lon_counts, wave_slots):
    lat_rows, level_rows, fields, longitudes = grid.shape
    slot_count = wave_slots.shape[0]
    degrees = legendre.shape[1]
    own_slots = legendre.shape[0]
    forward_table = forward_build(wave_slots, longitudes)
    own_counts = lax.dynamic_slice_in_dim(lon_counts, lax.axis_index("lat") * lat_rows, lat_rows)
    fourier = jnp.einsum("mrx,alfx->mralf", forward_table, grid, preferred_element_type=jnp.float32)
    fourier = fourier.reshape(slot_count, 2, lat_rows, level_rows * fields)
    forward_kept = (2 * wave_slots[:, None] < own_counts[None, :]).astype(jnp.float32)
    fourier = (fourier * forward_kept[:, None, :, None]).astype(jnp.bfloat16)
    gathered = lax.all_to_all(
        lax.all_to_all(fourier, "lat", split_axis=0, concat_axis=2, tiled=True),
        "lev",
        split_axis=0,
        concat_axis=3,
        tiled=True,
    )
    count = gathered.shape[0]
    own_table = lax.dynamic_slice_in_dim(legendre, lax.axis_index("lev") * count, count, 0)
    own_waves = lax.dynamic_slice_in_dim(
        wave_slots, lax.axis_index("lat") * own_slots + lax.axis_index("lev") * count, count
    )
    spectral = legendre_forward(own_table, gathered, own_waves)
    all_rows, all_damping = sent_together((vertical, damping), "lev", 0, 1)
    levels = all_rows.shape[0]
    stacked = spectral.reshape(count, degrees, 2, levels, fields)
    mixed = stacked.astype(jnp.float32) + jnp.einsum(
        "snrkf,lk->snrlf", stacked, all_rows, preferred_element_type=jnp.float32
    )
    mixed = mixed * damping_factor(degrees, all_damping)[None, :, None, :, None]
    mixed = mixed.astype(jnp.bfloat16).reshape(count, degrees, 2, levels * fields)
    banded = legendre_inverse(own_table, mixed)
    returned = joined_exchange(banded, ("lat", "lev"), ("lat", "lev"), (2, 3), (0, 0))
    back_order = (
        wave_slots.reshape(lax.axis_size("lat"), lax.axis_size("lev"), count)
        .transpose(1, 0, 2)
        .reshape(slot_count)
    )
    inverse_table = inverse_build(back_order, longitudes)
    back_kept = (2 * back_order[:, None] < own_counts[None, :]).astype(jnp.bfloat16)
    returned = returned * back_kept[:, None, :, None]
    filtered_grid = jnp.einsum(
        "mrac,mrx->acx", returned, inverse_table, preferred_element_type=jnp.float32
    )
    return filtered_grid.reshape(lat_rows, level_rows, fields, longitudes).astype(jnp.bfloat16)


def solution(mesh):
    return jax.shard_map(
        per_device,
        mesh=mesh,
        in_specs=(
            P("lat", "lev", None, None),
            P("lat", None, None),
            P("lev", None),
            P("lev"),
            P(),
            P(),
        ),
        out_specs=P("lat", "lev", None, None),
        check_vma=False,
    )
```

profile of v0, /device:TPU:3, one launch (start us, length us, event | category | flops | bytes accessed | tf_op | source)
XLA Modules:
  0.0 534.7 jit_solution(11057568427985806592)
XLA Ops:
  0.0 15.9 %multiply_convert_fusion.5 = (bf16[640,1,1280]{2,0,1:T(8,128)(2,1)S(1)}, bf16[640,1,1280]{2,0,1:T(8,128)(2,1)S(1)}) fusion(s32[640]{0:T(1024)} %param.11), kind=kLoop, calls=%fused_computation.38 | loop fusion | flops 11468800 | bytes 3279360 | tf_op jit(solution)/shard_map/convert.3
  15.9 0.9 reshape.395
  16.9 12.1 %fusion.2 = f32[640,2,20,32,4]{0,3,4,2,1:T(8,128)S(1)} fusion(bf16[20,32,4,1280]{3,2,1,0:T(4,128)(2,1)} %param.6, bf16[640,1,1280]{2,0,1:T(8,128)(2,1)S(1)} %get-tuple-element.12, bf16[640,1,1280]{2,0,1:T(8,128)(2,1)S(1)} %get-tuple-element.11), kind=kOutput, calls=%fused_computation.8 | convolution fusion | flops 8395161600 | bytes 22937600 | tf_op jit(solution)/shard_map/mrx,alfx->mralf/dot_general | solution.py:90
  29.0 0.0 copy-start
  29.0 15.4 %copy.70 = f32[640,2,20,32,4]{0,1,4,3,2:T(2,128)} copy(f32[640,2,20,32,4]{0,3,4,2,1:T(8,128)S(1)} %fusion.2) | data formatting | bytes 26214400 | tf_op jit(solution)/shard_map/mrx,alfx->mralf/dot_general | solution.py:90
  44.4 0.2 broadcast_in_dim_reshape.4
  44.6 0.0 copy-done
  44.7 0.8 dynamic_slice.10
  45.4 0.1 compare_convert_fusion
  45.5 7.9 %multiply_convert_fusion.1 = bf16[640,2,20,128]{0,1,3,2:T(2,128)(2,1)} fusion(f32[640,2,20,128]{0,1,3,2:T(2,128)} %bitcast.64, f32[640,20]{0,1:T(8,128)S(1)} %get-tuple-element.14), kind=kLoop, calls=%fused_computation.5 | loop fusion | flops 6553600 | bytes 19712000 | tf_op jit(solution)/shard_map/convert_element_type | solution.py:93
  53.5 22.8 %copy.71 = bf16[640,2,20,128]{3,1,2,0:T(2,128)(2,1)} copy(bf16[640,2,20,128]{0,1,3,2:T(2,128)(2,1)} %multiply_convert_fusion.1) | data formatting | bytes 13107200 | tf_op jit(solution)/shard_map/convert_element_type | solution.py:93
  76.3 84.1 %all_to_all.41 = bf16[640,2,20,128]{3,1,2,0:T(2,128)(2,1)S(1)} all-to-all(bf16[640,2,20,128]{3,1,2,0:T(2,128)(2,1)} %copy.71), channel_id=1, replica_groups=mesh['lat'=32,'lev'=4] {'lat'}, dimensions={0} | all-to-all | bytes 13107200 | tf_op jit(solution)/shard_map/all_to_all | solution.py:95
  160.4 5.8 %copy.72 = bf16[20,2,32,20,128]{4,1,3,2,0:T(2,128)(2,1)} copy(bf16[20,2,32,20,128]{4,1,3,0,2:T(2,128)(2,1)S(1)} %bitcast.69) | data formatting | bytes 13107200 | tf_op jit(solution)/shard_map/all_to_all | solution.py:95
  166.3 0.0 copy-start.2
  166.3 0.0 copy-start.1
  166.3 5.4 %all-to-all-start.1 = ((bf16[20,2,640,128]{3,1,2,0:T(2,128)(2,1)}), bf16[20,2,640,128]{3,1,2,0:T(2,128)(2,1)}, u32[]{:S(2)}, u32[]{:S(2)}) async-start(bf16[20,2,640,128]{3,1,2,0:T(2,128)(2,1)} %bitcast.65), calls=%async_computation.1 | async-start | bytes 13107200 | tf_op jit(solution)/shard_map/all_to_all | solution.py:94
  171.7 0.1 dynamic_slice.11
  171.8 0.0 copy-done.2
  171.8 0.1 copy.76
  171.9 0.0 copy-done.1
  171.9 77.4 %all_gather.3 = bf16[128,129]{1,0:T(8,128)(2,1)S(1)} all-gather(bf16[32,129]{1,0:T(8,128)(2,1)S(1)} %pad_maximum_fusion.1), channel_id=1, replica_groups=mesh['lat'=32,'lev'=4] {'lev'}, dimensions={0}, use_global_device_ids=true | all-gather | bytes 41280 | tf_op jit(solution)/shard_map/all_gather | solution.py:13
  249.3 0.1 convert_reduce_fusion
  249.4 0.1 fusion.29
  249.4 0.1 add_divide_fusion
  249.6 0.0 all-to-all-done.1
  249.6 7.2 %copy.73 = bf16[20,2,640,128]{3,2,1,0:T(8,128)(2,1)} copy(bf16[20,2,640,128]{3,1,2,0:T(2,128)(2,1)} %all-to-all-done.1) | data formatting | bytes 13107200 | tf_op jit(solution)/shard_map/all_to_all | solution.py:94
  256.8 9.5 %copy.74 = bf16[5,2,640,4,128]{2,4,3,1,0:T(8,128)(2,1)} copy(bf16[5,2,640,4,128]{4,2,1,0,3:T(8,128)(2,1)} %bitcast.70) | data formatting | bytes 13107200 | tf_op jit(solution)/shard_map/all_to_all | solution.py:94
  266.3 11.1 %multiply_convert_fusion = bf16[5,640,2,512]{1,3,2,0:T(8,128)(2,1)} fusion(bf16[5,2,640,512]{2,3,1,0:T(8,128)(2,1)} %bitcast.72, f32[5,640]{1,0:T(8,128)S(1)} %fusion.29, bf16[20,640,640]{2,1,0:T(8,128)(2,1)} %param.7, s32[]{:T(128)S(6)} %select_n.50), kind=kOutput, calls=%fused_computation.4 | convolution fusion | flops 4200857600 | bytes 17216004 | tf_op jit(solution)/shard_map/sna,srac->snrc/dot_general | solution.py:71
  277.4 11.8 %reshape.389 = bf16[5,640,2,128,4]{1,4,3,2,0:T(4,128)(2,1)} reshape(bf16[5,640,2,512]{1,3,2,0:T(8,128)(2,1)} %multiply_convert_fusion) | data formatting | bytes 13107200 | tf_op jit(solution)/shard_map/reshape | solution.py:109
  289.2 7.9 %fusion.1 = bf16[5,640,2,128,4]{1,3,4,2,0:T(8,128)(2,1)S(1)} fusion(bf16[5,640,2,128,4]{1,4,3,2,0:T(4,128)(2,1)} %reshape.389, f32[640,128]{0,1:T(8,128)S(1)} %add_divide_fusion, bf16[128,129]{1,0:T(8,128)(2,1)S(1)} %all_gather.3), kind=kOutput, calls=%fused_computation.3 | convolution fusion | flops 851968000 | bytes 20021248 | tf_op jit(solution)/shard_map/snrkf,lk->snrlf/dot_general | solution.py:110
  297.1 28.2 %copy.78 = bf16[5,640,2,128,4]{1,2,4,3,0:T(2,128)(2,1)S(1)} copy(bf16[5,640,2,128,4]{1,3,4,2,0:T(8,128)(2,1)S(1)} %fusion.1) | data formatting | bytes 13107200 | tf_op jit(solution)/shard_map/convert_element_type | solution.py:114
  325.3 10.1 %convert_bitcast_fusion = bf16[5,2,640,512]{2,3,1,0:T(8,128)(2,1)} fusion(bf16[5,640,2,512]{1,2,3,0:T(2,128)(2,1)S(1)} %bitcast.73, bf16[20,640,640]{2,1,0:T(8,128)(2,1)} %param.7, s32[]{:T(128)S(6)} %select_n.50), kind=kOutput, calls=%fused_computation.15 | convolution fusion | flops 4197580800 | bytes 17203204 | tf_op jit(solution)/shard_map/sna,snrc->srac/dot_general | solution.py:79
  335.4 16.7 %copy.80 = bf16[5,2,640,512]{3,1,2,0:T(2,128)(2,1)} copy(bf16[5,2,640,512]{2,3,1,0:T(8,128)(2,1)} %convert_bitcast_fusion) | data formatting | bytes 13107200 | tf_op jit(solution)/shard_map/convert_element_type | solution.py:80
  352.1 7.1 %fusion.36 = (bf16[32,5,2,20,128]{4,2,3,0,1:T(2,128)(2,1)S(1)}, bf16[32,5,2,20,128]{4,2,3,0,1:T(2,128)(2,1)S(1)}, bf16[32,5,2,20,128]{4,2,3,0,1:T(2,128)(2,1)S(1)}, bf16[32,5,2,20,128]{4,2,3,0,1:T(2,128)(2,1)S(1)}) fusion(bf16[32,5,2,20,512]{4,2,3,0,1:T(2,128)(2,1)} %bitcast.67), kind=kLoop, calls=%fused_computation.62 | loop fusion | bytes 13107200 | tf_op jit(solution)/shard_map/slice
  359.2 11.0 %pad_maximum_fusion = bf16[32,20,2,20,128]{4,2,3,0,1:T(2,128)(2,1)S(1)} fusion(bf16[32,5,2,20,128]{4,2,3,0,1:T(2,128)(2,1)S(1)} %get-tuple-element.6, bf16[32,5,2,20,128]{4,2,3,0,1:T(2,128)(2,1)S(1)} %get-tuple-element.7, bf16[32,5,2,20,128]{4,2,3,0,1:T(2,128)(2,1)S(1)} %get-tuple-element.8, bf16[32,5,2,20,128]{4,2,3,0,1:T(2,128)(2,1)S(1)} %get-tuple-element.5), kind=kLoop, calls=%fused_computation.6 | loop fusion | flops 9830400 | bytes 13107200 | tf_op jit(solution)/shard_map/concatenate
  370.2 5.9 %copy.81 = bf16[32,20,2,20,128]{4,2,3,1,0:T(2,128)(2,1)} copy(bf16[32,20,2,20,128]{4,2,3,0,1:T(2,128)(2,1)S(1)} %pad_maximum_fusion) | data formatting | bytes 13107200 | tf_op jit(solution)/shard_map/concatenate
  376.0 8.1 %all-to-all-start.2 = ((bf16[128,5,2,20,128]{4,2,3,1,0:T(2,128)(2,1)}), bf16[128,5,2,20,128]{4,2,3,1,0:T(2,128)(2,1)}, u32[]{:S(2)}, u32[]{:S(2)}) async-start(bf16[128,5,2,20,128]{4,2,3,1,0:T(2,128)(2,1)} %bitcast.66), calls=%async_computation.2 | async-start | bytes 13107200 | tf_op jit(solution)/shard_map/all_to_all | solution.py:37
  384.2 0.2 copy.84
  384.4 15.2 %multiply_convert_fusion.3 = (bf16[640,1,1280]{2,0,1:T(8,128)(2,1)S(1)}, bf16[640,1,1280]{2,0,1:T(8,128)(2,1)S(1)}) fusion(f32[640]{0:T(1024)S(1)} %select_multiply_fusion, s32[640]{0:T(1024)S(1)} %broadcast_in_dim_reshape.4), kind=kLoop, calls=%fused_computation.33 | loop fusion | flops 11468800 | bytes 3281920 | tf_op jit(solution)/shard_map/convert.1
  399.5 63.9 %all-to-all-done.2 = bf16[128,5,2,20,128]{4,2,3,1,0:T(2,128)(2,1)} async-done(((bf16[128,5,2,20,128]{4,2,3,1,0:T(2,128)(2,1)}), bf16[128,5,2,20,128]{4,2,3,1,0:T(2,128)(2,1)}, u32[]{:S(2)}, u32[]{:S(2)}) %all-to-all-start.2) | async-done | bytes 6553632 | tf_op jit(solution)/shard_map/all_to_all | solution.py:37
  463.4 6.0 %copy.82 = bf16[32,4,5,2,20,128]{5,3,4,2,0,1:T(2,128)(2,1)S(1)} copy(bf16[32,4,5,2,20,128]{5,3,4,2,1,0:T(2,128)(2,1)} %bitcast.22) | data formatting | bytes 13107200 | tf_op jit(solution)/shard_map/reshape | solution.py:38
  469.5 17.0 %bitcast_multiply_fusion = bf16[640,2,20,128]{3,1,2,0:T(2,128)(2,1)} fusion(bf16[32,4,5,2,20,128]{5,3,4,2,0,1:T(2,128)(2,1)S(1)} %copy.82, bf16[640,20]{1,0:T(8,128)(2,1)S(1)} %copy.84), kind=kLoop, calls=%fused_computation.7 | loop fusion | flops 3276800 | bytes 13132800 | tf_op jit(solution)/shard_map/mul | solution.py:124
  486.5 23.5 %copy.85 = bf16[20,128,640,2]{2,3,1,0:T(2,128)(2,1)} copy(bf16[20,128,640,2]{1,3,0,2:T(2,128)(2,1)} %bitcast.68) | data formatting | bytes 13107200 | tf_op jit(solution)/shard_map/mrac,mrx->acx/dot_general | solution.py:125
  510.0 13.3 %bitcast_convert_fusion = bf16[20,32,4,1280]{3,1,2,0:T(8,128)(2,1)} fusion(bf16[20,32,4,640,2]{3,4,2,1,0:T(2,128)(2,1)} %bitcast.71, bf16[640,1,1280]{2,0,1:T(8,128)(2,1)S(1)} %get-tuple-element.10, bf16[640,1,1280]{2,0,1:T(8,128)(2,1)S(1)} %get-tuple-element.9), kind=kOutput, calls=%fused_computation | convolution fusion | flops 8393523200 | bytes 16384000 | tf_op jit(solution)/shard_map/mrac,mrx->acx/dot_general | solution.py:125
  523.3 11.4 %copy.87 = bf16[20,32,4,1280]{3,2,1,0:T(4,128)(2,1)} copy(bf16[20,32,4,1280]{3,1,2,0:T(8,128)(2,1)} %bitcast_convert_fusion) | data formatting | bytes 13107200 | tf_op jit(solution)/shard_map/convert_element_type | solution.py:128
  (5 shorter events, 0.0 us)
Async XLA Ops:
  29.0 15.6 %copy-start = (s32[640]{0:T(1024)S(1)}, s32[640]{0:T(1024)}, u32[]{:S(2)}) copy-start(s32[640]{0:T(1024)} %param.11) | copy-start | bytes 7684
  166.3 5.5 %copy-start.2 = (bf16[32]{0:T(256)(128)(2,1)S(1)}, bf16[32]{0:T(256)(128)(2,1)}, u32[]{:S(2)}) copy-start(bf16[32]{0:T(256)(128)(2,1)} %param.9) | copy-start | bytes 196
  166.3 5.6 %copy-start.1 = (bf16[32,128]{1,0:T(8,128)(2,1)S(1)}, bf16[32,128]{1,0:T(8,128)(2,1)}, u32[]{:S(2)}) copy-start(bf16[32,128]{1,0:T(8,128)(2,1)} %param.8) | copy-start | bytes 24580
  166.3 83.3 %all-to-all-start.1 = ((bf16[20,2,640,128]{3,1,2,0:T(2,128)(2,1)}), bf16[20,2,640,128]{3,1,2,0:T(2,128)(2,1)}, u32[]{:S(2)}, u32[]{:S(2)}) async-start(bf16[20,2,640,128]{3,1,2,0:T(2,128)(2,1)} %bitcast.65), calls=%async_computation.1 | async-start | bytes 13107200 | tf_op jit(solution)/shard_map/all_to_all | solution.py:94
  376.0 87.4 %all-to-all-start.2 = ((bf16[128,5,2,20,128]{4,2,3,1,0:T(2,128)(2,1)}), bf16[128,5,2,20,128]{4,2,3,1,0:T(2,128)(2,1)}, u32[]{:S(2)}, u32[]{:S(2)}) async-start(bf16[128,5,2,20,128]{4,2,3,1,0:T(2,128)(2,1)} %bitcast.66), calls=%async_computation.2 | async-start | bytes 13107200 | tf_op jit(solution)/shard_map/all_to_all | solution.py:37
where the time goes:
time: 537 us; the launch traced here: 535 us
  local copies, waits for them, and re-layouts  174 us (32%)
  blocking collectives  162 us (30%)
  other arithmetic  67.4 us (13%)
  waiting for transfers between devices  63.9 us (12%)
  matrix products  54.5 us (10%)
  starting transfers between devices  13.6 us (3%)
    all_to_all x1, blocking collectives, per_device(): lax.all_to_all(fourier, 'lat', split_axis=0, concat_axis=2, tiled=True)  84.1 us
    all_gather x1, blocking collectives, sent_together(): result = lax.all_gather(both, axis, axis=dim, tiled=True)  77.4 us
    all_to_all x1, waiting for transfers between devices, joined_exchange(): lax.all_to_all(pieces, axis, split_axis=0, concat_axis=0, tiled=True)  63.9 us
    another operation x2, other arithmetic  31.1 us
    convert_element_type x1, local copies, waits for them, and re-layouts, per_device(): mixed.astype(jnp.bfloat16).reshape(count, degrees, 2, levels * fields)  28.2 us
    dot_general x1, local copies, waits for them, and re-layouts, per_device(): jnp.einsum('mrac,mrx->acx', returned, inverse_table, preferred_element_ty...  23.5 us
    convert_element_type x1, local copies, waits for them, and re-layouts, per_device(): fourier = (fourier * forward_kept[:, None, :, None]).astype(jnp.bfloat16)  22.8 us
    mul x1, other arithmetic, per_device(): returned = returned * back_kept[:, None, :, None]  17 us
  transfers between devices with their start and end apart: 2, of which 1 were waited for; matrix products, arithmetic and copies ran while one was open for 3% of the time, Pallas kernels for 0%

commit v1 on v0

--- a/solution.py
+++ b/solution.py
@@ -91,12 +91,20 @@
     fourier = fourier.reshape(slot_count, 2, lat_rows, level_rows * fields)
     forward_kept = (2 * wave_slots[:, None] < own_counts[None, :]).astype(jnp.float32)
     fourier = (fourier * forward_kept[:, None, :, None]).astype(jnp.bfloat16)
-    gathered = lax.all_to_all(
-        lax.all_to_all(fourier, "lat", split_axis=0, concat_axis=2, tiled=True),
-        "lev",
-        split_axis=0,
-        concat_axis=3,
-        tiled=True,
+    gathered = jnp.concatenate(
+        lax.all_to_all(
+            jnp.stack(
+                jnp.split(
+                    lax.all_to_all(fourier, "lat", split_axis=0, concat_axis=2, tiled=True),
+                    lax.axis_size("lev"),
+                    axis=0,
+                )
+            ),
+            "lev",
+            0,
+            0,
+        ),
+        axis=3,
     )
     count = gathered.shape[0]
     own_table = lax.dynamic_slice_in_dim(legendre, lax.axis_index("lev") * count, count, 0)

time: 537 us -> 564 us (1.050); the launches traced: 535 us -> 555 us
  other arithmetic: 67.4 us -> 83.6 us
    all_to_all x3 -> x0, local copies, waits for them, and re-layouts: 22.5 us -> none  [the longest x2 16.7 us: per_device(): lax.all_to_all(lax.all_to_all(fourier, 'lat', split_axis=0, concat_axis=2...]
    reshape x0 -> x1, local copies, waits for them, and re-layouts: none -> 16.7 us  [per_device(): jnp.concatenate(lax.all_to_all(jnp.stack(jnp.split(lax.all_to_all(fourier...]
    another operation x2 -> x3, other arithmetic: 31.1 us -> 47.3 us
    split x0 -> x5, local copies, waits for them, and re-layouts: none -> 9.15 us  [per_device(): jnp.split(lax.all_to_all(fourier, 'lat', split_axis=0, concat_axis=2, til...]
    another operation x0 -> x1, local copies, waits for them, and re-layouts: none -> 7.1 us
    slice x1 -> x0, local copies, waits for them, and re-layouts: 7.1 us -> none
where the time goes in v1:
time: 564 us; the launch traced here: 555 us
  local copies, waits for them, and re-layouts  177 us (31%)
  blocking collectives  162 us (29%)
  other arithmetic  83.6 us (15%)
  waiting for transfers between devices  63.9 us (11%)
  matrix products  54.5 us (10%)
  starting transfers between devices  13.9 us (2%)
    all_to_all x1, blocking collectives, per_device(): lax.all_to_all(fourier, 'lat', split_axis=0, concat_axis=2, tiled=True)  84.4 us
    all_gather x1, blocking collectives, sent_together(): result = lax.all_gather(both, axis, axis=dim, tiled=True)  77.4 us
    all_to_all x1, waiting for transfers between devices, joined_exchange(): lax.all_to_all(pieces, axis, split_axis=0, concat_axis=0, tiled=True)  63.9 us
    another operation x2, other arithmetic  31.1 us
    convert_element_type x1, local copies, waits for them, and re-layouts, per_device(): mixed.astype(jnp.bfloat16).reshape(count, degrees, 2, levels * fields)  28.2 us
    dot_general x1, local copies, waits for them, and re-layouts, per_device(): jnp.einsum('mrac,mrx->acx', returned, inverse_table, preferred_element_ty...  23.5 us
    convert_element_type x1, local copies, waits for them, and re-layouts, per_device(): fourier = (fourier * forward_kept[:, None, :, None]).astype(jnp.bfloat16)  22.9 us
    mul x1, other arithmetic, per_device(): returned = returned * back_kept[:, None, :, None]  17 us
  transfers between devices with their start and end apart: 2, of which 1 were waited for; matrix products, arithmetic and copies ran while one was open for 3% of the time, Pallas kernels for 0%

profile of v1, /device:TPU:3, one launch (start us, length us, event | category | flops | bytes accessed | tf_op | source)
XLA Modules:
  0.0 555.2 jit_solution(17559517252346941394)
XLA Ops:
  0.0 15.9 %multiply_convert_fusion.5 = (bf16[640,1,1280]{2,0,1:T(8,128)(2,1)S(1)}, bf16[640,1,1280]{2,0,1:T(8,128)(2,1)S(1)}) fusion(s32[640]{0:T(1024)} %param.11), kind=kLoop, calls=%fused_computation.39 | loop fusion | flops 11468800 | bytes 3279360 | tf_op jit(solution)/shard_map/convert.3
  15.9 0.9 reshape.411
  16.9 12.1 %fusion.2 = f32[640,2,20,32,4]{0,3,4,2,1:T(8,128)S(1)} fusion(bf16[20,32,4,1280]{3,2,1,0:T(4,128)(2,1)} %param.6, bf16[640,1,1280]{2,0,1:T(8,128)(2,1)S(1)} %get-tuple-element.16, bf16[640,1,1280]{2,0,1:T(8,128)(2,1)S(1)} %get-tuple-element.15), kind=kOutput, calls=%fused_computation.9 | convolution fusion | flops 8395161600 | bytes 22937600 | tf_op jit(solution)/shard_map/mrx,alfx->mralf/dot_general | solution.py:90
  29.0 0.0 copy-start
  29.0 15.5 %copy.56 = f32[640,2,20,32,4]{0,1,4,3,2:T(2,128)} copy(f32[640,2,20,32,4]{0,3,4,2,1:T(8,128)S(1)} %fusion.2) | data formatting | bytes 26214400 | tf_op jit(solution)/shard_map/mrx,alfx->mralf/dot_general | solution.py:90
  44.5 0.2 broadcast_in_dim_reshape.4
  44.7 0.0 copy-done
  44.7 0.8 dynamic_slice.10
  45.5 0.1 compare_convert_fusion
  45.6 7.9 %multiply_convert_fusion.1 = bf16[640,2,20,128]{0,1,3,2:T(2,128)(2,1)} fusion(f32[640,2,20,128]{0,1,3,2:T(2,128)} %bitcast.65, f32[640,20]{0,1:T(8,128)S(1)} %get-tuple-element.18), kind=kLoop, calls=%fused_computation.5 | loop fusion | flops 6553600 | bytes 19712000 | tf_op jit(solution)/shard_map/convert_element_type | solution.py:93
  53.5 22.9 %copy.57 = bf16[640,2,20,128]{3,1,2,0:T(2,128)(2,1)} copy(bf16[640,2,20,128]{0,1,3,2:T(2,128)(2,1)} %multiply_convert_fusion.1) | data formatting | bytes 13107200 | tf_op jit(solution)/shard_map/convert_element_type | solution.py:93
  76.4 84.4 %all_to_all.25 = bf16[640,2,20,128]{3,1,2,0:T(2,128)(2,1)S(1)} all-to-all(bf16[640,2,20,128]{3,1,2,0:T(2,128)(2,1)} %copy.57), channel_id=1, replica_groups=mesh['lat'=32,'lev'=4] {'lat'}, dimensions={0} | all-to-all | bytes 13107200 | tf_op jit(solution)/shard_map/all_to_all | solution.py:98
  160.8 4.6 fusion.37
  165.5 1.1 copy.61
  166.6 1.1 copy.60
  167.7 1.1 copy.59
  168.9 1.1 copy.58
  170.0 16.2 %pad_maximum_fusion = bf16[4,5,2,640,128]{4,2,3,1,0:T(2,128)(2,1)} fusion(bf16[1,5,2,640,128]{4,2,3,1,0:T(2,128)(2,1)S(1)} %bitcast.70, bf16[1,5,2,640,128]{4,2,3,1,0:T(2,128)(2,1)S(1)} %bitcast.71, bf16[1,5,2,640,128]{4,2,3,1,0:T(2,128)(2,1)S(1)} %bitcast.72, bf16[1,5,2,640,128]{4,2,3,1,0:T(2,128)(2,1)S(1)} %bitcast.73), kind=kLoop, calls=%fused_computation.6 | loop fusion | flops 9830400 | bytes 13107200 | tf_op jit(solution)/shard_map/stack | solution.py:96
  186.2 0.0 copy-start.2
  186.2 0.0 copy-start.1
  186.2 5.4 all-to-all-start.1
  191.6 0.1 dynamic_slice.11
  191.7 0.0 copy-done.2
  191.7 0.1 copy.64
  191.8 0.0 copy-done.1
  191.8 77.4 %all_gather.3 = bf16[128,129]{1,0:T(8,128)(2,1)S(1)} all-gather(bf16[32,129]{1,0:T(8,128)(2,1)S(1)} %pad_maximum_fusion.2), channel_id=1, replica_groups=mesh['lat'=32,'lev'=4] {'lev'}, dimensions={0}, use_global_device_ids=true | all-gather | bytes 41280 | tf_op jit(solution)/shard_map/all_gather | solution.py:13
  269.2 0.1 convert_reduce_fusion
  269.3 0.1 fusion.29
  269.4 0.1 add_divide_fusion
  269.5 0.0 all-to-all-done.1
  269.5 16.7 %copy.62 = bf16[5,2,640,4,128]{2,4,3,1,0:T(8,128)(2,1)} copy(bf16[5,2,640,4,128]{4,1,2,0,3:T(2,128)(2,1)} %bitcast.13) | data formatting | bytes 13107200 | tf_op jit(solution)/shard_map/reshape | solution.py:94
  286.2 11.1 %multiply_convert_fusion = bf16[5,640,2,512]{1,3,2,0:T(8,128)(2,1)} fusion(bf16[5,2,640,512]{2,3,1,0:T(8,128)(2,1)} %bitcast.75, f32[5,640]{1,0:T(8,128)S(1)} %fusion.29, bf16[20,640,640]{2,1,0:T(8,128)(2,1)} %param.7, s32[]{:T(128)S(6)} %select_n.50), kind=kOutput, calls=%fused_computation.4 | convolution fusion | flops 4200857600 | bytes 17216004 | tf_op jit(solution)/shard_map/sna,srac->snrc/dot_general | solution.py:71
  297.3 11.8 %reshape.405 = bf16[5,640,2,128,4]{1,4,3,2,0:T(4,128)(2,1)} reshape(bf16[5,640,2,512]{1,3,2,0:T(8,128)(2,1)} %multiply_convert_fusion) | data formatting | bytes 13107200 | tf_op jit(solution)/shard_map/reshape | solution.py:117
  309.1 7.9 %fusion.1 = bf16[5,640,2,128,4]{1,3,4,2,0:T(8,128)(2,1)S(1)} fusion(bf16[5,640,2,128,4]{1,4,3,2,0:T(4,128)(2,1)} %reshape.405, f32[640,128]{0,1:T(8,128)S(1)} %add_divide_fusion, bf16[128,129]{1,0:T(8,128)(2,1)S(1)} %all_gather.3), kind=kOutput, calls=%fused_computation.3 | convolution fusion | flops 851968000 | bytes 20021248 | tf_op jit(solution)/shard_map/snrkf,lk->snrlf/dot_general | solution.py:118
  316.9 28.2 %copy.66 = bf16[5,640,2,128,4]{1,2,4,3,0:T(2,128)(2,1)S(1)} copy(bf16[5,640,2,128,4]{1,3,4,2,0:T(8,128)(2,1)S(1)} %fusion.1) | data formatting | bytes 13107200 | tf_op jit(solution)/shard_map/convert_element_type | solution.py:122
  345.2 10.1 %convert_bitcast_fusion = bf16[5,2,640,512]{2,3,1,0:T(8,128)(2,1)} fusion(bf16[5,640,2,512]{1,2,3,0:T(2,128)(2,1)S(1)} %bitcast.76, bf16[20,640,640]{2,1,0:T(8,128)(2,1)} %param.7, s32[]{:T(128)S(6)} %select_n.50), kind=kOutput, calls=%fused_computation.16 | convolution fusion | flops 4197580800 | bytes 17203204 | tf_op jit(solution)/shard_map/sna,snrc->srac/dot_general | solution.py:79
  355.3 16.7 %copy.68 = bf16[5,2,640,512]{3,1,2,0:T(2,128)(2,1)} copy(bf16[5,2,640,512]{2,3,1,0:T(8,128)(2,1)} %convert_bitcast_fusion) | data formatting | bytes 13107200 | tf_op jit(solution)/shard_map/convert_element_type | solution.py:80
  372.0 7.1 %fusion.36 = (bf16[32,5,2,20,128]{4,2,3,0,1:T(2,128)(2,1)S(1)}, bf16[32,5,2,20,128]{4,2,3,0,1:T(2,128)(2,1)S(1)}, bf16[32,5,2,20,128]{4,2,3,0,1:T(2,128)(2,1)S(1)}, bf16[32,5,2,20,128]{4,2,3,0,1:T(2,128)(2,1)S(1)}) fusion(bf16[32,5,2,20,512]{4,2,3,0,1:T(2,128)(2,1)} %bitcast.68), kind=kLoop, calls=%fused_computation.63 | loop fusion | bytes 13107200 | tf_op jit(solution)/shard_map/slice.4
  379.1 11.0 %pad_maximum_fusion.1 = bf16[32,20,2,20,128]{4,2,3,0,1:T(2,128)(2,1)S(1)} fusion(bf16[32,5,2,20,128]{4,2,3,0,1:T(2,128)(2,1)S(1)} %get-tuple-element.6, bf16[32,5,2,20,128]{4,2,3,0,1:T(2,128)(2,1)S(1)} %get-tuple-element.7, bf16[32,5,2,20,128]{4,2,3,0,1:T(2,128)(2,1)S(1)} %get-tuple-element.8, bf16[32,5,2,20,128]{4,2,3,0,1:T(2,128)(2,1)S(1)} %get-tuple-element.5), kind=kLoop, calls=%fused_computation.7 | loop fusion | flops 9830400 | bytes 13107200 | tf_op jit(solution)/shard_map/concatenate
  390.1 5.9 %copy.69 = bf16[32,20,2,20,128]{4,2,3,1,0:T(2,128)(2,1)} copy(bf16[32,20,2,20,128]{4,2,3,0,1:T(2,128)(2,1)S(1)} %pad_maximum_fusion.1) | data formatting | bytes 13107200 | tf_op jit(solution)/shard_map/concatenate
  396.0 8.5 %all-to-all-start.2 = ((bf16[128,5,2,20,128]{4,2,3,1,0:T(2,128)(2,1)}), bf16[128,5,2,20,128]{4,2,3,1,0:T(2,128)(2,1)}, u32[]{:S(2)}, u32[]{:S(2)}) async-start(bf16[128,5,2,20,128]{4,2,3,1,0:T(2,128)(2,1)} %bitcast.66), calls=%async_computation.2 | async-start | bytes 13107200 | tf_op jit(solution)/shard_map/all_to_all | solution.py:37
  404.5 0.2 copy.72
  404.7 15.2 %multiply_convert_fusion.3 = (bf16[640,1,1280]{2,0,1:T(8,128)(2,1)S(1)}, bf16[640,1,1280]{2,0,1:T(8,128)(2,1)S(1)}) fusion(f32[640]{0:T(1024)S(1)} %select_multiply_fusion, s32[640]{0:T(1024)S(1)} %broadcast_in_dim_reshape.4), kind=kLoop, calls=%fused_computation.34 | loop fusion | flops 11468800 | bytes 3281920 | tf_op jit(solution)/shard_map/convert.1
  419.8 63.9 %all-to-all-done.2 = bf16[128,5,2,20,128]{4,2,3,1,0:T(2,128)(2,1)} async-done(((bf16[128,5,2,20,128]{4,2,3,1,0:T(2,128)(2,1)}), bf16[128,5,2,20,128]{4,2,3,1,0:T(2,128)(2,1)}, u32[]{:S(2)}, u32[]{:S(2)}) %all-to-all-start.2) | async-done | bytes 6553632 | tf_op jit(solution)/shard_map/all_to_all | solution.py:37
  483.7 6.0 %copy.70 = bf16[32,4,5,2,20,128]{5,3,4,2,0,1:T(2,128)(2,1)S(1)} copy(bf16[32,4,5,2,20,128]{5,3,4,2,1,0:T(2,128)(2,1)} %bitcast.25) | data formatting | bytes 13107200 | tf_op jit(solution)/shard_map/reshape | solution.py:38
  489.7 17.0 %bitcast_multiply_fusion = bf16[640,2,20,128]{3,1,2,0:T(2,128)(2,1)} fusion(bf16[32,4,5,2,20,128]{5,3,4,2,0,1:T(2,128)(2,1)S(1)} %copy.70, bf16[640,20]{1,0:T(8,128)(2,1)S(1)} %copy.72), kind=kLoop, calls=%fused_computation.8 | loop fusion | flops 3276800 | bytes 13132800 | tf_op jit(solution)/shard_map/mul | solution.py:132
  506.7 23.5 %copy.73 = bf16[20,128,640,2]{2,3,1,0:T(2,128)(2,1)} copy(bf16[20,128,640,2]{1,3,0,2:T(2,128)(2,1)} %bitcast.69) | data formatting | bytes 13107200 | tf_op jit(solution)/shard_map/mrac,mrx->acx/dot_general | solution.py:133
  530.2 13.4 %bitcast_convert_fusion = bf16[20,32,4,1280]{3,1,2,0:T(8,128)(2,1)} fusion(bf16[20,32,4,640,2]{3,4,2,1,0:T(2,128)(2,1)} %bitcast.74, bf16[640,1,1280]{2,0,1:T(8,128)(2,1)S(1)} %get-tuple-element.14, bf16[640,1,1280]{2,0,1:T(8,128)(2,1)S(1)} %get-tuple-element.13), kind=kOutput, calls=%fused_computation | convolution fusion | flops 8393523200 | bytes 16384000 | tf_op jit(solution)/shard_map/mrac,mrx->acx/dot_general | solution.py:133
  543.6 11.4 %copy.75 = bf16[20,32,4,1280]{3,2,1,0:T(4,128)(2,1)} copy(bf16[20,32,4,1280]{3,1,2,0:T(8,128)(2,1)} %bitcast_convert_fusion) | data formatting | bytes 13107200 | tf_op jit(solution)/shard_map/convert_element_type | solution.py:136
  (5 shorter events, 0.0 us)
Async XLA Ops:
  29.0 15.7 %copy-start = (s32[640]{0:T(1024)S(1)}, s32[640]{0:T(1024)}, u32[]{:S(2)}) copy-start(s32[640]{0:T(1024)} %param.11) | copy-start | bytes 7684
  186.2 5.5 copy-start.2
  186.2 5.6 %copy-start.1 = (bf16[32,128]{1,0:T(8,128)(2,1)S(1)}, bf16[32,128]{1,0:T(8,128)(2,1)}, u32[]{:S(2)}) copy-start(bf16[32,128]{1,0:T(8,128)(2,1)} %param.8) | copy-start | bytes 24580
  186.2 83.3 %all-to-all-start.1 = ((bf16[4,5,2,640,128]{4,2,3,1,0:T(2,128)(2,1)}), bf16[4,5,2,640,128]{4,2,3,1,0:T(2,128)(2,1)}, u32[]{:S(2)}, u32[]{:S(2)}) async-start(bf16[4,5,2,640,128]{4,2,3,1,0:T(2,128)(2,1)} %pad_maximum_fusion), calls=%async_computation.1 | async-start | bytes 13107200 | tf_op jit(solution)/shard_map/all_to_all | solution.py:95
  396.0 87.7 %all-to-all-start.2 = ((bf16[128,5,2,20,128]{4,2,3,1,0:T(2,128)(2,1)}), bf16[128,5,2,20,128]{4,2,3,1,0:T(2,128)(2,1)}, u32[]{:S(2)}, u32[]{:S(2)}) async-start(bf16[128,5,2,20,128]{4,2,3,1,0:T(2,128)(2,1)} %bitcast.66), calls=%async_computation.2 | async-start | bytes 13107200 | tf_op jit(solution)/shard_map/all_to_all | solution.py:37
